TPU v7x, 32 devices: a whole 2x2x4 slice. The times are simulated.
32 devices in a mesh: inst: 2 (over x), qy: 4 (over z), qx: 4 (over y, core).
Axes of the slice: x: 2, y: 2, z: 4, core: 2. Of those that a mesh axis runs over, the one named last changes fastest.
Arguments:
- cost_diag: float32 [8388608], P(('inst', 'qx', 'qy')), parts along dimension 0
- gammas: float32 [4], replicated
- betas: float32 [4], replicated
Outputs:
- output 1: float32 [2], P('inst'), parts along dimension 0
- output 2: float32 [8388608], P(('inst', 'qx', 'qy')), parts along dimension 0
- output 3: float32 [8388608], P(('inst', 'qx', 'qy')), parts along dimension 0
There are 2 independent parts. A program takes and returns all parts, laid end to end along the dimension named above; an argument that names none is the same for every part.
All inputs are finite; a program needn't handle non-finite values.
Results may differ from a plain program's by a relative error of at most 0.001.
Values sent between devices are 32-bit elements.
A program may use at most 1 GiB of HBM per device.

v0:
```python
import math
import jax
import jax.numpy as jnp
from jax import lax
from jax.sharding import PartitionSpec as P

LANES = 128


def quarter_turn(state_pair):
    sign_pair = jnp.array([1.0, -1.0], jnp.float32).reshape(2, 1, 1)
    return jnp.flip(state_pair, axis=0) * sign_pair


def flip_bit(state_pair, qubit_id):
    if qubit_id < 7:
        axis_id = 2
        bit_step = 1 << qubit_id
    else:
        axis_id = 1
        bit_step = 1 << (qubit_id - 7)
    extent = state_pair.shape[axis_id]
    iota_shape = [1, 1, 1]
    iota_shape[axis_id] = extent
    position = lax.broadcasted_iota(jnp.int32, tuple(iota_shape), axis_id)
    bit_set = (position & bit_step) != 0
    return jnp.where(bit_set, jnp.roll(state_pair, bit_step, axis=axis_id),
                     jnp.roll(state_pair, -bit_step, axis=axis_id))


def local_mixer(state_pair, cos_half, sin_half, qubit_ids):
    for qubit_id in qubit_ids:
        partner = flip_bit(state_pair, qubit_id)
        state_pair = cos_half * state_pair + sin_half * quarter_turn(partner)
    return state_pair


def global_mixer(state_pair, cos_half, sin_half, axis_name, axis_size):
    for bit_id in range(int(math.log2(axis_size))):
        bit_step = 1 << bit_id
        perm_pairs = [(source_id, source_id ^ bit_step) for source_id in range(axis_size)]
        partner = lax.ppermute(state_pair, axis_name, perm_pairs)
        state_pair = cos_half * state_pair + sin_half * quarter_turn(partner)
    return state_pair


def solution(mesh):
    size_x = mesh.shape['qx']
    size_y = mesh.shape['qy']
    state_spec = P(('inst', 'qx', 'qy'))

    def device_body(cost_local, gammas, betas):
        local_len = cost_local.shape[0]
        local_qubits = int(math.log2(local_len))
        row_count = local_len // LANES
        cost_rows = cost_local.reshape(row_count, LANES)
        state_pair = jnp.stack([jnp.ones((row_count, LANES), jnp.float32),
                                jnp.zeros((row_count, LANES), jnp.float32)])
        for layer_id in range(gammas.shape[0]):
            phase_angle = gammas[layer_id] * cost_rows
            state_pair = jnp.cos(phase_angle) * state_pair + jnp.sin(phase_angle) * quarter_turn(state_pair)
            cos_half = jnp.cos(0.5 * betas[layer_id])
            sin_half = jnp.sin(0.5 * betas[layer_id])
            state_pair = local_mixer(state_pair, cos_half, sin_half, range(local_qubits))
            state_pair = global_mixer(state_pair, cos_half, sin_half, 'qy', size_y)
            state_pair = global_mixer(state_pair, cos_half, sin_half, 'qx', size_x)
        local_energy = jnp.sum(cost_rows * (state_pair[0] * state_pair[0] + state_pair[1] * state_pair[1]))
        energy = lax.psum(local_energy, ('qx', 'qy')) / (local_len * size_x * size_y)
        return energy.reshape(1), state_pair[0].reshape(local_len), state_pair[1].reshape(local_len)

    return jax.shard_map(device_body, mesh=mesh, in_specs=(state_spec, P(), P()),
                         out_specs=(P('inst'), state_spec, state_spec), check_vma=False)
```

profile of v0, /device:TPU:0, one launch (start us, length us, event | category | flops | bytes accessed | tf_op | source)
XLA Modules:
  0.0 973.4 jit_solution(11708663056857449144)
XLA Ops:
  0.6 1.5 fusion.137
  2.1 19.1 %cosine_bitcast_fusion.3 = (f32[2048,128]{1,0:T(8,128)}, f32[2048,128]{1,0:T(8,128)}, f32[2048,128]{1,0:T(8,128)}, f32[2048,128]{1,0:T(8,128)S(1)}, f32[2048,128...) fusion(f32[262144]{0:T(1024)} %param.95, f32[]{:T(128)} %bitcast.1, ...), kind=kLoop, calls=%fused_computation.174 | loop fusion | flops 1048576 | bytes 9437200 | tf_op jit(solution)/shard_map/cos | solution.py:61
  25.1 1.1 maximum_select_fusion
  31.6 1.1 maximum_select_fusion.2
  34.4 1.5 maximum_select_fusion.3
  40.5 1.1 maximum_select_fusion.5
  59.1 3.2 collective-permute-start
  62.2 45.6 %collective-permute-done = f32[2,2048,128]{2,1,0:T(8,128)S(1)} collective-permute-done((f32[2,2048,128]{2,1,0:T(8,128)S(1)}, f32[2,2048,128]{2,1,0:T(8,128)S(1)}, u32[]{:S(2)}, u32[]{:S(2)}) %collective-permute-start) | collective-permute-done | bytes 2097184 | tf_op jit(solution)/shard_map/ppermute | solution.py:42
  108.2 2.8 collective-permute-start.1
  111.1 89.8 %collective-permute-done.1 = f32[2,2048,128]{2,1,0:T(8,128)S(1)} collective-permute-done((f32[2,2048,128]{2,1,0:T(8,128)S(1)}, f32[2,2048,128]{2,1,0:T(8,128)S(1)}, u32[]{:S(2)}, u32[]{:S(2)}) %collective-permute-start.1) | collective-permute-done | bytes 2097184 | tf_op jit(solution)/shard_map/ppermute | solution.py:42
  201.3 4.1 collective-permute-done.2
  205.9 1.5 collective-permute-start.3
  208.1 45.6 %collective-permute-done.3 = f32[2,2048,128]{2,1,0:T(8,128)S(1)} collective-permute-done((f32[2,2048,128]{2,1,0:T(8,128)S(1)}, f32[2,2048,128]{2,1,0:T(8,128)S(1)}, u32[]{:S(2)}, u32[]{:S(2)}) %collective-permute-start.3) | collective-permute-done | bytes 2097184 | tf_op jit(solution)/shard_map/ppermute | solution.py:42
  255.7 1.1 maximum_select_fusion.16
  264.7 1.1 maximum_select_fusion.19
  267.6 1.1 maximum_select_fusion.20
  270.4 1.1 maximum_select_fusion.21
  275.6 1.5 maximum_select_fusion.23
  289.8 46.3 %collective-permute-done.4 = f32[2,2048,128]{2,1,0:T(8,128)S(1)} collective-permute-done((f32[2,2048,128]{2,1,0:T(8,128)S(1)}, f32[2,2048,128]{2,1,0:T(8,128)S(1)}, u32[]{:S(2)}, u32[]{:S(2)}) %collective-permute-start.4) | collective-permute-done | bytes 2097184 | tf_op jit(solution)/shard_map/ppermute | solution.py:42
  336.5 2.2 collective-permute-start.5
  338.7 89.6 %collective-permute-done.5 = f32[2,2048,128]{2,1,0:T(8,128)S(1)} collective-permute-done((f32[2,2048,128]{2,1,0:T(8,128)S(1)}, f32[2,2048,128]{2,1,0:T(8,128)S(1)}, u32[]{:S(2)}, u32[]{:S(2)}) %collective-permute-start.5) | collective-permute-done | bytes 2097184 | tf_op jit(solution)/shard_map/ppermute | solution.py:42
  428.7 4.1 collective-permute-done.6
  433.2 1.5 collective-permute-start.7
  435.4 45.5 %collective-permute-done.7 = f32[2,2048,128]{2,1,0:T(8,128)S(1)} collective-permute-done((f32[2,2048,128]{2,1,0:T(8,128)S(1)}, f32[2,2048,128]{2,1,0:T(8,128)S(1)}, u32[]{:S(2)}, u32[]{:S(2)}) %collective-permute-start.7) | collective-permute-done | bytes 2097184 | tf_op jit(solution)/shard_map/ppermute | solution.py:42
  483.1 1.1 maximum_select_fusion.32
  486.2 1.1 maximum_select_fusion.33
  489.0 1.1 maximum_select_fusion.34
  492.1 1.1 maximum_select_fusion.35
  494.9 1.1 maximum_select_fusion.36
  497.7 1.1 maximum_select_fusion.37
  502.9 1.5 maximum_select_fusion.39
  517.1 46.4 %collective-permute-done.8 = f32[2,2048,128]{2,1,0:T(8,128)S(1)} collective-permute-done((f32[2,2048,128]{2,1,0:T(8,128)S(1)}, f32[2,2048,128]{2,1,0:T(8,128)S(1)}, u32[]{:S(2)}, u32[]{:S(2)}) %collective-permute-start.8) | collective-permute-done | bytes 2097184 | tf_op jit(solution)/shard_map/ppermute | solution.py:42
  563.8 2.2 collective-permute-start.9
  566.0 89.6 %collective-permute-done.9 = f32[2,2048,128]{2,1,0:T(8,128)S(1)} collective-permute-done((f32[2,2048,128]{2,1,0:T(8,128)S(1)}, f32[2,2048,128]{2,1,0:T(8,128)S(1)}, u32[]{:S(2)}, u32[]{:S(2)}) %collective-permute-start.9) | collective-permute-done | bytes 2097184 | tf_op jit(solution)/shard_map/ppermute | solution.py:42
  656.0 4.1 collective-permute-done.10
  660.5 1.5 collective-permute-start.11
  662.8 45.4 %collective-permute-done.11 = f32[2,2048,128]{2,1,0:T(8,128)S(1)} collective-permute-done((f32[2,2048,128]{2,1,0:T(8,128)S(1)}, f32[2,2048,128]{2,1,0:T(8,128)S(1)}, u32[]{:S(2)}, u32[]{:S(2)}) %collective-permute-start.11) | collective-permute-done | bytes 2097184 | tf_op jit(solution)/shard_map/ppermute | solution.py:42
  710.4 1.1 maximum_select_fusion.48
  719.4 1.1 maximum_select_fusion.51
  730.3 1.3 maximum_select_fusion.55
  744.1 46.4 %collective-permute-done.12 = f32[2,2048,128]{2,1,0:T(8,128)S(1)} collective-permute-done((f32[2,2048,128]{2,1,0:T(8,128)S(1)}, f32[2,2048,128]{2,1,0:T(8,128)S(1)}, u32[]{:S(2)}, u32[]{:S(2)}) %collective-permute-start.12) | collective-permute-done | bytes 2097184 | tf_op jit(solution)/shard_map/ppermute | solution.py:42
  790.8 2.2 collective-permute-start.13
  793.0 89.6 %collective-permute-done.13 = f32[2,2048,128]{2,1,0:T(8,128)S(1)} collective-permute-done((f32[2,2048,128]{2,1,0:T(8,128)S(1)}, f32[2,2048,128]{2,1,0:T(8,128)S(1)}, u32[]{:S(2)}, u32[]{:S(2)}) %collective-permute-start.13) | collective-permute-done | bytes 2097184 | tf_op jit(solution)/shard_map/ppermute | solution.py:42
  883.0 4.1 collective-permute-done.14
  887.5 1.5 collective-permute-start.15
  889.0 46.3 %collective-permute-done.15 = f32[2,2048,128]{2,1,0:T(8,128)S(1)} collective-permute-done((f32[2,2048,128]{2,1,0:T(8,128)S(1)}, f32[2,2048,128]{2,1,0:T(8,128)S(1)}, u32[]{:S(2)}, u32[]{:S(2)}) %collective-permute-start.15) | collective-permute-done | bytes 2097184 | tf_op jit(solution)/shard_map/ppermute | solution.py:42
  935.6 2.1 multiply_reduce_fusion
  937.8 33.4 %psum.7 = f32[]{:T(128)} all-reduce(f32[]{:T(128)} %get-tuple-element.3), channel_id=1, replica_groups=mesh['inst'=2,'qy'=4,'qx'=4] {'qx','qy'}, use_global_device_ids=true, to_apply=%region_1.2 | all-reduce | flops 1 | bytes 8 | tf_op jit(solution)/shard_map/psum | solution.py:68
  (322 shorter events, 125.4 us)
Async XLA Ops:
  2.1 19.1 %copy-start.7 = (f32[2]{0:T(128)S(1)}, f32[2]{0:T(128)}, u32[]{:S(2)}) copy-start(f32[2]{0:T(128)} %constant.17.clone.1) | copy-start | bytes 28
  21.2 0.7 copy-start.4
  22.9 0.7 copy-start.6
  59.1 48.8 %collective-permute-start = (f32[2,2048,128]{2,1,0:T(8,128)S(1)}, f32[2,2048,128]{2,1,0:T(8,128)S(1)}, u32[]{:S(2)}, u32[]{:S(2)}) collective-permute-start(f32[2,2048,128]{2,1,0:T(8,128)S(1)} %multiply_add_fusion.73), channel_id=1, source_target_pairs={{0,4},{4,0},{8,12},{12,8},{1,5},{5,1},{9,13},{13,9},{2,6},{6,2},{1... | collective-permute-start | bytes 6291464 | tf_op jit(solution)/shard_map/ppermute | solution.py:42
  108.2 92.6 %collective-permute-start.1 = (f32[2,2048,128]{2,1,0:T(8,128)S(1)}, f32[2,2048,128]{2,1,0:T(8,128)S(1)}, u32[]{:S(2)}, u32[]{:S(2)}) collective-permute-start(f32[2,2048,128]{2,1,0:T(8,128)S(1)} %multiply_add_fusion.72), channel_id=1, source_target_pairs={{0,8},{4,12},{8,0},{12,4},{1,9},{5,13},{9,1},{13,5},{2,10},{6,14},... | collective-permute-start | bytes 6291464 | tf_op jit(solution)/shard_map/ppermute | solution.py:42
  201.3 4.2 collective-permute-start.2
  205.9 47.7 %collective-permute-start.3 = (f32[2,2048,128]{2,1,0:T(8,128)S(1)}, f32[2,2048,128]{2,1,0:T(8,128)S(1)}, u32[]{:S(2)}, u32[]{:S(2)}) collective-permute-start(f32[2,2048,128]{2,1,0:T(8,128)S(1)} %multiply_add_fusion.70), channel_id=1, source_target_pairs={{0,2},{1,3},{2,0},{3,1},{4,6},{5,7},{6,4},{7,5},{8,10},{9,11},{10,... | collective-permute-start | bytes 6291464 | tf_op jit(solution)/shard_map/ppermute | solution.py:42
  289.2 46.9 %collective-permute-start.4 = (f32[2,2048,128]{2,1,0:T(8,128)S(1)}, f32[2,2048,128]{2,1,0:T(8,128)S(1)}, u32[]{:S(2)}, u32[]{:S(2)}) collective-permute-start(f32[2,2048,128]{2,1,0:T(8,128)S(1)} %multiply_add_fusion.50), channel_id=1, source_target_pairs={{0,4},{4,0},{8,12},{12,8},{1,5},{5,1},{9,13},{13,9},{2,6},{6,2},{1... | collective-permute-start | bytes 6291464 | tf_op jit(solution)/shard_map/ppermute | solution.py:42
  336.5 91.8 %collective-permute-start.5 = (f32[2,2048,128]{2,1,0:T(8,128)S(1)}, f32[2,2048,128]{2,1,0:T(8,128)S(1)}, u32[]{:S(2)}, u32[]{:S(2)}) collective-permute-start(f32[2,2048,128]{2,1,0:T(8,128)S(1)} %multiply_add_fusion.49), channel_id=1, source_target_pairs={{0,8},{4,12},{8,0},{12,4},{1,9},{5,13},{9,1},{13,5},{2,10},{6,14},... | collective-permute-start | bytes 6291464 | tf_op jit(solution)/shard_map/ppermute | solution.py:42
  428.6 4.2 collective-permute-start.6
  433.2 47.7 %collective-permute-start.7 = (f32[2,2048,128]{2,1,0:T(8,128)S(1)}, f32[2,2048,128]{2,1,0:T(8,128)S(1)}, u32[]{:S(2)}, u32[]{:S(2)}) collective-permute-start(f32[2,2048,128]{2,1,0:T(8,128)S(1)} %multiply_add_fusion.47), channel_id=1, source_target_pairs={{0,2},{1,3},{2,0},{3,1},{4,6},{5,7},{6,4},{7,5},{8,10},{9,11},{10,... | collective-permute-start | bytes 6291464 | tf_op jit(solution)/shard_map/ppermute | solution.py:42
  435.4 45.9 %copy-start.2 = (f32[2048,128]{1,0:T(8,128)S(1)}, f32[2048,128]{1,0:T(8,128)}, u32[]{:S(2)}) copy-start(f32[2048,128]{1,0:T(8,128)} %get-tuple-element.280) | copy-start | bytes 3145732
  435.4 45.9 %copy-start.3 = (f32[2048,128]{1,0:T(8,128)S(1)}, f32[2048,128]{1,0:T(8,128)}, u32[]{:S(2)}) copy-start(f32[2048,128]{1,0:T(8,128)} %get-tuple-element.284) | copy-start | bytes 3145732
  516.6 46.9 %collective-permute-start.8 = (f32[2,2048,128]{2,1,0:T(8,128)S(1)}, f32[2,2048,128]{2,1,0:T(8,128)S(1)}, u32[]{:S(2)}, u32[]{:S(2)}) collective-permute-start(f32[2,2048,128]{2,1,0:T(8,128)S(1)} %multiply_add_fusion.27), channel_id=1, source_target_pairs={{0,4},{4,0},{8,12},{12,8},{1,5},{5,1},{9,13},{13,9},{2,6},{6,2},{1... | collective-permute-start | bytes 6291464 | tf_op jit(solution)/shard_map/ppermute | solution.py:42
  563.8 91.8 %collective-permute-start.9 = (f32[2,2048,128]{2,1,0:T(8,128)S(1)}, f32[2,2048,128]{2,1,0:T(8,128)S(1)}, u32[]{:S(2)}, u32[]{:S(2)}) collective-permute-start(f32[2,2048,128]{2,1,0:T(8,128)S(1)} %multiply_add_fusion.26), channel_id=1, source_target_pairs={{0,8},{4,12},{8,0},{12,4},{1,9},{5,13},{9,1},{13,5},{2,10},{6,14},... | collective-permute-start | bytes 6291464 | tf_op jit(solution)/shard_map/ppermute | solution.py:42
  655.9 4.2 collective-permute-start.10
  660.5 47.7 %collective-permute-start.11 = (f32[2,2048,128]{2,1,0:T(8,128)S(1)}, f32[2,2048,128]{2,1,0:T(8,128)S(1)}, u32[]{:S(2)}, u32[]{:S(2)}) collective-permute-start(f32[2,2048,128]{2,1,0:T(8,128)S(1)} %multiply_add_fusion.24), channel_id=1, source_target_pairs={{0,2},{1,3},{2,0},{3,1},{4,6},{5,7},{6,4},{7,5},{8,10},{9,11},{10,... | collective-permute-start | bytes 6291464 | tf_op jit(solution)/shard_map/ppermute | solution.py:42
  662.8 45.8 %copy-start = (f32[2048,128]{1,0:T(8,128)S(1)}, f32[2048,128]{1,0:T(8,128)}, u32[]{:S(2)}) copy-start(f32[2048,128]{1,0:T(8,128)} %get-tuple-element.278) | copy-start | bytes 3145732
  662.8 45.8 %copy-start.1 = (f32[2048,128]{1,0:T(8,128)S(1)}, f32[2048,128]{1,0:T(8,128)}, u32[]{:S(2)}) copy-start(f32[2048,128]{1,0:T(8,128)} %get-tuple-element.279) | copy-start | bytes 3145732
  743.6 46.9 %collective-permute-start.12 = (f32[2,2048,128]{2,1,0:T(8,128)S(1)}, f32[2,2048,128]{2,1,0:T(8,128)S(1)}, u32[]{:S(2)}, u32[]{:S(2)}) collective-permute-start(f32[2,2048,128]{2,1,0:T(8,128)S(1)} %multiply_add_fusion.4), channel_id=1, source_target_pairs={{0,4},{4,0},{8,12},{12,8},{1,5},{5,1},{9,13},{13,9},{2,6},{6,2},{1... | collective-permute-start | bytes 6291464 | tf_op jit(solution)/shard_map/ppermute | solution.py:42
  790.8 91.8 %collective-permute-start.13 = (f32[2,2048,128]{2,1,0:T(8,128)S(1)}, f32[2,2048,128]{2,1,0:T(8,128)S(1)}, u32[]{:S(2)}, u32[]{:S(2)}) collective-permute-start(f32[2,2048,128]{2,1,0:T(8,128)S(1)} %multiply_add_fusion.3), channel_id=1, source_target_pairs={{0,8},{4,12},{8,0},{12,4},{1,9},{5,13},{9,1},{13,5},{2,10},{6,14},... | collective-permute-start | bytes 6291464 | tf_op jit(solution)/shard_map/ppermute | solution.py:42
  882.9 4.2 collective-permute-start.14
  887.5 48.1 %copy-start.5 = (f32[262144]{0:T(1024)S(1)}, f32[262144]{0:T(1024)}, u32[]{:S(2)}) copy-start(f32[262144]{0:T(1024)} %param.95) | copy-start | bytes 3145732
  887.5 47.7 %collective-permute-start.15 = (f32[2,2048,128]{2,1,0:T(8,128)S(1)}, f32[2,2048,128]{2,1,0:T(8,128)S(1)}, u32[]{:S(2)}, u32[]{:S(2)}) collective-permute-start(f32[2,2048,128]{2,1,0:T(8,128)S(1)} %multiply_add_fusion.1), channel_id=1, source_target_pairs={{0,2},{1,3},{2,0},{3,1},{4,6},{5,7},{6,4},{7,5},{8,10},{9,11},{10,... | collective-permute-start | bytes 6291464 | tf_op jit(solution)/shard_map/ppermute | solution.py:42
where the time goes:
time: 983 us; the launch traced here: 973 us
  waiting for transfers between devices  743 us (76%)
  other arithmetic  120 us (12%)
  local copies, waits for them, and re-layouts  49.6 us (5%)
  blocking collectives  33.4 us (3%)
  starting transfers between devices  20.3 us (2%)
    ppermute x16, waiting for transfers between devices, global_mixer(): partner = lax.ppermute(state_pair, axis_name, perm_pairs)  743 us
    select_n x64, other arithmetic, flip_bit(): jnp.where(bit_set, jnp.roll(state_pair, bit_step, axis=axis_id), jnp.roll...  60.3 us
    slice x128, local copies, waits for them, and re-layouts, flip_bit(): jnp.roll(state_pair, -bit_step, axis=axis_id)  43.6 us
    psum x1, blocking collectives, device_body(): lax.psum(local_energy, ('qx', 'qy')) / (local_len * size_x * size_y)  33.4 us
    add x72, other arithmetic, local_mixer(): state_pair = cos_half * state_pair + sin_half * quarter_turn(partner)  27.5 us
    ppermute x16, starting transfers between devices, global_mixer(): partner = lax.ppermute(state_pair, axis_name, perm_pairs)  20.3 us
  transfers between devices with their start and end apart: 16, of which 16 were waited for; matrix products, arithmetic and copies ran while one was open for 0% of the time, Pallas kernels for 0%

commit v1 on v0

v1 whole, which is shorter than its diff:
```python
import functools
import jax
import jax.numpy as jnp
from jax import lax
from jax.experimental import pallas as pl
from jax.experimental.pallas import tpu as pltpu
from jax.sharding import PartitionSpec as P

MESH = pl.DeviceIdType.MESH
LAYERS = 4
BLOCKS = 16
ROWS = 128
LANES = 128
GROUPS = ((2, 3, 6, 7), (10, 11, 14, 15), (1, 5, 9, 13), (12, 8, 4, 0))
HIGHEST = lax.Precision.HIGHEST


def flip(bits, mask):
    new = [1 - b if (mask >> i) & 1 else b for i, b in enumerate(bits)]
    qy = new[0] + 2 * new[1]
    qx = new[2] + 2 * new[3]
    return 4 * qx + qy, {'qx': qx, 'qy': qy}


def gates(vals, cos_half, sin_half):
    vals = list(vals)
    for bit in range(4):
        step = 1 << bit
        for low in range(BLOCKS):
            if low & step:
                continue
            (ar, ai), (br, bi) = vals[low], vals[low + step]
            vals[low] = (cos_half * ar + sin_half * bi, cos_half * ai - sin_half * br)
            vals[low + step] = (cos_half * br + sin_half * ai, cos_half * bi - sin_half * ar)
    return vals


def kernel(size, cost_ref, gam_ref, bet_ref, en_ref, re_ref, im_ref, cost_b, work, snd, rcv, tab, mix, half, part,
           cs_sem, cr_sem, ss_sem, sr_sem, es_sem, er_sem):
    qx, qy = lax.axis_index('qx'), lax.axis_index('qy')
    bits = [lax.rem(qy, 2), lax.div(qy, 2), lax.rem(qx, 2), lax.div(qx, 2)]
    me = 4 * qx + qy

    barrier = pltpu.get_barrier_semaphore()
    for mask in range(1, BLOCKS):
        pl.semaphore_signal(barrier, inc=1, device_id=flip(bits, mask)[1], device_id_type=MESH)
    pl.semaphore_wait(barrier, BLOCKS - 1)

    def copies(src, dst, send_sem, recv_sem, mask):
        peer, where = flip(bits, mask)
        return pltpu.make_async_remote_copy(src_ref=src(peer), dst_ref=dst, send_sem=send_sem.at[mask],
                                            recv_sem=recv_sem.at[mask], device_id=where, device_id_type=MESH)

    cost_copies = [copies(lambda peer: cost_ref.at[peer], cost_b.at[me], cs_sem, cr_sem, mask)
                   for group in GROUPS for mask in group if mask]
    for copy in cost_copies:
        copy.start()
    cost_b[me] = cost_ref[me]

    ri = lax.broadcasted_iota(jnp.int32, (ROWS, LANES), 0)
    ci = lax.broadcasted_iota(jnp.int32, (ROWS, LANES), 1)
    diff = ri ^ ci
    dist = diff & 1
    for i in range(1, 7):
        dist = dist + ((diff >> i) & 1)
    for layer in range(LAYERS):
        angle = jnp.full((8, LANES), bet_ref[layer], jnp.float32) * 0.5
        half[layer, 0] = jnp.cos(angle)
        half[layer, 1] = jnp.sin(angle)
        c = half[layer, 0, 0:1, :]
        s = half[layer, 1, 0:1, :]
        cp, sp = [jnp.ones_like(c)], [jnp.ones_like(s)]
        for _ in range(7):
            cp.append(cp[-1] * c)
            sp.append(sp[-1] * s)
        real = jnp.zeros((ROWS, LANES), jnp.float32)
        imag = jnp.zeros((ROWS, LANES), jnp.float32)
        for d in range(8):
            term = cp[7 - d] * sp[d]
            if d % 4 in (1, 2):
                term = -term
            term = jnp.broadcast_to(term, (ROWS, LANES))
            if d % 2 == 0:
                real = jnp.where(dist == d, term, real)
            else:
                imag = jnp.where(dist == d, term, imag)
        mix[layer, 0:128, 0:128] = real
        mix[layer, 0:128, 128:256] = imag
        mix[layer, 128:256, 0:128] = -imag
        mix[layer, 128:256, 128:256] = real

    def table(layer, load):
        gamma = gam_ref[layer]

        def fill(k, carry):
            angle = gamma * load(k)
            tab[layer, k, :, 0:128] = jnp.cos(angle)
            tab[layer, k, :, 128:256] = jnp.sin(angle)
            return carry

        lax.fori_loop(0, BLOCKS, fill, 0)

    def top_first():
        c, s = half[0, 0], half[0, 1]

        def rows(r, carry):
            at = pl.ds(pl.multiple_of(r * 8, 8), 8)
            vals = [(tab[0, k, at, 0:128], -tab[0, k, at, 128:256]) for k in range(BLOCKS)]
            vals = gates(vals, c, s)
            for k in range(BLOCKS):
                work[k, at, 0:128] = vals[k][0]
                work[k, at, 128:256] = vals[k][1]
            return carry

        lax.fori_loop(0, ROWS // 8, rows, 0)

    def top(layer):
        c0, s0, c1, s1 = half[layer - 1, 0], half[layer - 1, 1], half[layer, 0], half[layer, 1]

        def rows(r, carry):
            at = pl.ds(pl.multiple_of(r * 8, 8), 8)
            vals = [(rcv[layer - 1, k, at, 0:128], rcv[layer - 1, k, at, 128:256]) for k in range(BLOCKS)]
            vals = gates(vals, c0, s0)
            for k in range(BLOCKS):
                re, im = vals[k]
                pc, ps = tab[layer, k, at, 0:128], tab[layer, k, at, 128:256]
                vals[k] = (re * pc + im * ps, im * pc - re * ps)
            vals = gates(vals, c1, s1)
            for k in range(BLOCKS):
                work[k, at, 0:128] = vals[k][0]
                work[k, at, 128:256] = vals[k][1]
            return carry

        lax.fori_loop(0, ROWS // 8, rows, 0)

    def low_and_send(layer):
        started = []
        for group in GROUPS:
            index = [flip(bits, mask)[0] for mask in group]
            x = jnp.concatenate([work[k] for k in index], axis=0)
            y = jnp.dot(x, mix[layer], precision=HIGHEST, preferred_element_type=jnp.float32)
            y = jnp.concatenate(
                [jnp.concatenate([y[i * 128:(i + 1) * 128, 0:128].T, y[i * 128:(i + 1) * 128, 128:256].T], axis=1)
                 for i in range(len(group))], axis=0)
            y = jnp.dot(y, mix[layer], precision=HIGHEST, preferred_element_type=jnp.float32)
            for i, mask in enumerate(group):
                if mask:
                    snd[layer, index[i]] = y[i * 128:(i + 1) * 128]
                else:
                    rcv[layer, me] = y[i * 128:(i + 1) * 128]
            for mask in group:
                if mask:
                    copy = copies(lambda peer: snd.at[layer, peer], rcv.at[layer, me], ss_sem.at[layer],
                                  sr_sem.at[layer], mask)
                    copy.start()
                    started.append(copy)
        return started

    table(0, lambda k: cost_ref[k])
    top_first()
    pending = low_and_send(0)
    table(2, lambda k: cost_ref[k])
    for copy in cost_copies:
        copy.wait()

    def turned(k):
        return cost_b[k].T

    table(1, turned)
    for layer in range(1, LAYERS):
        if layer == 2:
            table(3, turned)
        for copy in pending:
            copy.wait()
        top(layer)
        pending = low_and_send(layer)
    for copy in pending:
        copy.wait()

    last = LAYERS - 1
    c, s = half[last, 0], half[last, 1]

    def finish(r, acc):
        at = pl.ds(pl.multiple_of(r * 8, 8), 8)
        vals = gates([(rcv[last, k, at, 0:128], rcv[last, k, at, 128:256]) for k in range(BLOCKS)], c, s)
        for k in range(BLOCKS):
            re, im = vals[k]
            re_ref[k, at, :] = re
            im_ref[k, at, :] = im
            acc = acc + cost_ref[k, at, :] * (re * re + im * im)
        return acc

    part[me] = lax.fori_loop(0, ROWS // 8, finish, jnp.zeros((8, LANES), jnp.float32))
    sums = [copies(lambda peer: part.at[me], part.at[me], es_sem, er_sem, mask) for mask in range(1, BLOCKS)]
    for copy in sums:
        copy.start()
    for copy in sums:
        copy.wait()
    total = part[0]
    for k in range(1, BLOCKS):
        total = total + part[k]
    en_ref[0] = jnp.sum(total) / size


def solution(mesh):
    state_spec = P(('inst', 'qx', 'qy'))

    def device_body(cost_local, gammas, betas):
        local_len = cost_local.shape[0]
        size = local_len * mesh.shape['qx'] * mesh.shape['qy']
        block = (BLOCKS, ROWS, LANES)
        pair = (BLOCKS, ROWS, 2 * LANES)
        vmem = pl.BlockSpec(memory_space=pltpu.VMEM)
        smem = pl.BlockSpec(memory_space=pltpu.SMEM)
        dma = pltpu.SemaphoreType.DMA
        energy, state_re, state_im = pl.pallas_call(
            functools.partial(kernel, size),
            out_shape=(jax.ShapeDtypeStruct((1,), jnp.float32), jax.ShapeDtypeStruct(block, jnp.float32),
                       jax.ShapeDtypeStruct(block, jnp.float32)),
            in_specs=[vmem, smem, smem],
            out_specs=(smem, vmem, vmem),
            scratch_shapes=[
                pltpu.VMEM(block, jnp.float32),
                pltpu.VMEM(pair, jnp.float32),
                pltpu.VMEM((LAYERS,) + pair, jnp.float32),
                pltpu.VMEM((LAYERS,) + pair, jnp.float32),
                pltpu.VMEM((LAYERS,) + pair, jnp.float32),
                pltpu.VMEM((LAYERS, 2 * LANES, 2 * LANES), jnp.float32),
                pltpu.VMEM((LAYERS, 2, 8, LANES), jnp.float32),
                pltpu.VMEM((BLOCKS, 8, LANES), jnp.float32),
                dma((BLOCKS,)), dma((BLOCKS,)),
                dma((LAYERS, BLOCKS)), dma((LAYERS, BLOCKS)),
                dma((BLOCKS,)), dma((BLOCKS,)),
            ],
            compiler_params=pltpu.CompilerParams(collective_id=0, has_side_effects=True),
            name='qaoa',
        )(cost_local.reshape(block), gammas, betas)
        return energy, state_re.reshape(local_len), state_im.reshape(local_len)

    return jax.shard_map(device_body, mesh=mesh, in_specs=(state_spec, P(), P()),
                         out_specs=(P('inst'), state_spec, state_spec), check_vma=False)
```

time: 983 us -> 239 us (0.24)
  waiting for transfers between devices: 743 us -> 0 us
  Pallas kernels: 0 us -> 233 us
  other arithmetic: 120 us -> 0 us
  local copies, waits for them, and re-layouts: 49.6 us -> 3.39 us
  blocking collectives: 33.4 us -> 0 us
  starting transfers between devices: 20.3 us -> 0 us
    ppermute x16 -> x0, waiting for transfers between devices: 743 us -> none  [global_mixer(): partner = lax.ppermute(state_pair, axis_name, perm_pairs)]
    pallas_call x0 -> x1, Pallas kernels: none -> 233 us  [device_body(): pl.pallas_call(functools.partial(kernel, size), out_shape=(jax.ShapeDtype...]
    select_n x64 -> x0, other arithmetic: 60.3 us -> none  [flip_bit(): jnp.where(bit_set, jnp.roll(state_pair, bit_step, axis=axis_id), jnp.roll...]
    slice x138 -> x0, local copies, waits for them, and re-layouts: 48.9 us -> none  [the longest x128 43.6 us: flip_bit(): jnp.roll(state_pair, -bit_step, axis=axis_id)]
    add x92 -> x0, other arithmetic: 34.9 us -> none  [the longest x72 27.5 us: local_mixer(): state_pair = cos_half * state_pair + sin_half * quarter_turn(partner)]
    psum x1 -> x0, blocking collectives: 33.4 us -> none  [device_body(): lax.psum(local_energy, ('qx', 'qy')) / (local_len * size_x * size_y)]
    ppermute x16 -> x0, starting transfers between devices: 20.3 us -> none  [global_mixer(): partner = lax.ppermute(state_pair, axis_name, perm_pairs)]
    cos x1 -> x0, other arithmetic: 19.1 us -> none  [device_body(): jnp.cos(phase_angle) * state_pair]
  transfers between devices with their start and end apart: 16 -> 0, of which waited for: 16 -> 0; matrix products, arithmetic and copies ran while one was open for 0% -> 0% of each run, Pallas kernels for 0% -> 0%
where the time goes in v1:
time: 239 us
  Pallas kernels  233 us (97%)
  local copies, waits for them, and re-layouts  3.39 us (1%)
  between operations  2.39 us (1%)
    pallas_call x1, Pallas kernels, device_body(): pl.pallas_call(functools.partial(kernel, size), out_shape=(jax.ShapeDtype...  233 us

profile of v1, /device:TPU:0, one launch (start us, length us, event | category | flops | bytes accessed | tf_op | source)
XLA Modules:
  0.0 238.9 jit_solution(10638399526332889638)
XLA Ops:
  0.6 233.1 %qaoa.1 = (f32[1]{0:T(128)}, f32[16,128,128]{2,1,0:T(8,128)}, f32[16,128,128]{2,1,0:T(8,128)}) custom-call(f32[16,128,128]{2,1,0:T(8,128)} %bitcast.3, f32[4]{0:T(128)} %gam_ref.1, f32[4]{0:T(128)} %bet_ref.1), custom_call_target="tpu_custom_call" | custom-call | tf_op jit(solution)/shard_map/qaoa/pallas_call | solution.py:216
  234.4 0.0 copy-start
  234.4 2.4 copy.10
  236.7 0.0 copy-done
  236.7 1.0 copy.11
Async XLA Ops:
  234.4 2.4 copy-start

commit v2 on v1

--- a/solution.py
+++ b/solution.py
@@ -10,16 +10,13 @@
 LAYERS = 4
 BLOCKS = 16
 ROWS = 128
+HALF = ROWS // 2
 LANES = 128
-GROUPS = ((2, 3, 6, 7), (10, 11, 14, 15), (1, 5, 9, 13), (12, 8, 4, 0))
+CHUNKS = 8
+STEP = BLOCKS // CHUNKS
+GROUPS = ((2, 4, 8, 14), (6, 10, 12, 15), (3, 5, 9, 7), (11, 13, 1, 0))
+PAIRS = ((2, 3), (6, 7), (4, 5), (0, 1))
 HIGHEST = lax.Precision.HIGHEST
-
-
-def flip(bits, mask):
-    new = [1 - b if (mask >> i) & 1 else b for i, b in enumerate(bits)]
-    qy = new[0] + 2 * new[1]
-    qx = new[2] + 2 * new[3]
-    return 4 * qx + qy, {'qx': qx, 'qy': qy}
 
 
 def gates(vals, cos_half, sin_half):
@@ -35,27 +32,50 @@
     return vals
 
 
-def kernel(size, cost_ref, gam_ref, bet_ref, en_ref, re_ref, im_ref, cost_b, work, snd, rcv, tab, mix, half, part,
-           cs_sem, cr_sem, ss_sem, sr_sem, es_sem, er_sem):
-    qx, qy = lax.axis_index('qx'), lax.axis_index('qy')
-    bits = [lax.rem(qy, 2), lax.div(qy, 2), lax.rem(qx, 2), lax.div(qx, 2)]
-    me = 4 * qx + qy
+def kernel(size, cost_ref, gam_ref, bet_ref, en_ref, re_ref, im_ref, both, far, cost_b, work, snd, rcv, tab, mix, half,
+           part, xs_sem, xr_sem, zs_sem, zr_sem, cs_sem, cr_sem, ss_sem, sr_sem, fs_sem, fr_sem, es_sem, er_sem):
+    x, qx, qy = lax.axis_index('inst'), lax.axis_index('qx'), lax.axis_index('qy')
+    core, y = lax.rem(qx, 2), lax.div(qx, 2)
+    z0, h = lax.rem(qy, 2), lax.div(qy, 2)
+    home = 1 - (x + h - 2 * x * h)
+    cid = core + 2 * z0 + 4 * y + 8 * x
+
+    def pick(bit, mask, i):
+        return 1 - bit if (mask >> i) & 1 else bit
+
+    def cube_peer(mask):
+        c, z, v, u = pick(core, mask, 0), pick(z0, mask, 1), pick(y, mask, 2), pick(x, mask, 3)
+        return c + 2 * z + 4 * v + 8 * u, {'inst': u, 'qx': 2 * v + c, 'qy': 2 * h + z}
+
+    def plane_peer(mask, inst):
+        c, z, v, t = pick(core, mask, 0), pick(z0, mask, 1), pick(y, mask, 2), pick(h, mask, 3)
+        return c + 2 * z + 4 * v, t, {'inst': inst, 'qx': 2 * v + c, 'qy': 2 * t + z}
 
     barrier = pltpu.get_barrier_semaphore()
-    for mask in range(1, BLOCKS):
-        pl.semaphore_signal(barrier, inc=1, device_id=flip(bits, mask)[1], device_id_type=MESH)
-    pl.semaphore_wait(barrier, BLOCKS - 1)
-
-    def copies(src, dst, send_sem, recv_sem, mask):
-        peer, where = flip(bits, mask)
-        return pltpu.make_async_remote_copy(src_ref=src(peer), dst_ref=dst, send_sem=send_sem.at[mask],
-                                            recv_sem=recv_sem.at[mask], device_id=where, device_id_type=MESH)
-
-    cost_copies = [copies(lambda peer: cost_ref.at[peer], cost_b.at[me], cs_sem, cr_sem, mask)
-                   for group in GROUPS for mask in group if mask]
-    for copy in cost_copies:
+    for mask in range(2 * BLOCKS):
+        if mask:
+            inst = pick(x, mask, 4)
+            pl.semaphore_signal(barrier, inc=1, device_id=plane_peer(mask, inst)[2], device_id_type=MESH)
+    pl.semaphore_wait(barrier, 2 * BLOCKS - 1)
+
+    def remote(src, dst, send_sem, recv_sem, where):
+        return pltpu.make_async_remote_copy(src_ref=src, dst_ref=dst, send_sem=send_sem, recv_sem=recv_sem,
+                                            device_id=where, device_id_type=MESH)
+
+    here = pl.ds(pl.multiple_of(HALF * x, HALF), HALF)
+    there = pl.ds(pl.multiple_of(HALF * (1 - x), HALF), HALF)
+    slot_h = pl.ds(pl.multiple_of(HALF * h, HALF), HALF)
+    slot_f = pl.ds(pl.multiple_of(HALF * (1 - h), HALF), HALF)
+    x_copies, z_copies = [], []
+    for j in range(CHUNKS):
+        at = pl.ds(STEP * j, STEP)
+        x_copies.append(remote(cost_ref.at[at, there], both.at[0, at], xs_sem.at[j], xr_sem.at[j],
+                               {'inst': 1 - x, 'qx': qx, 'qy': qy}))
+        z_copies.append(remote(both.at[1 - home, at], far.at[at], zs_sem.at[j], zr_sem.at[j],
+                               {'inst': x, 'qx': qx, 'qy': 2 * (1 - h) + z0}))
+    for copy in x_copies:
         copy.start()
-    cost_b[me] = cost_ref[me]
+    both[1] = cost_ref[:, here, :]
 
     ri = lax.broadcasted_iota(jnp.int32, (ROWS, LANES), 0)
     ci = lax.broadcasted_iota(jnp.int32, (ROWS, LANES), 1)
@@ -89,16 +109,44 @@
         mix[layer, 128:256, 0:128] = -imag
         mix[layer, 128:256, 128:256] = real
 
-    def table(layer, load):
+    def table(layer, load, rows, first, count):
         gamma = gam_ref[layer]
 
         def fill(k, carry):
             angle = gamma * load(k)
-            tab[layer, k, :, 0:128] = jnp.cos(angle)
-            tab[layer, k, :, 128:256] = jnp.sin(angle)
+            tab[layer, k, rows, 0:128] = jnp.cos(angle)
+            tab[layer, k, rows, 128:256] = jnp.sin(angle)
             return carry
 
-        lax.fori_loop(0, BLOCKS, fill, 0)
+        lax.fori_loop(first, first + count, fill, 0)
+
+    def block_to(d):
+        return {'inst': d >> 3, 'qx': 2 * ((d >> 2) & 1) + (d & 1), 'qy': 2 * h + ((d >> 1) & 1)}
+
+    def pass_on(src, d, rows, which):
+        @pl.when(cid != d)
+        def _():
+            remote(src.at[d], cost_b.at[cid, rows], cs_sem.at[which, d], cr_sem.at[which, cid], block_to(d)).start()
+
+    def keep(k):
+        return both[home, k]
+
+    def distant(k):
+        return far[k]
+
+    for j in range(CHUNKS):
+        x_copies[j].wait_recv()
+        z_copies[j].start()
+        for d in range(STEP * j, STEP * (j + 1)):
+            pass_on(both.at[home], d, slot_h, 0)
+    table(0, keep, slot_h, 0, BLOCKS)
+    for j in range(CHUNKS):
+        z_copies[j].wait_recv()
+        for d in range(STEP * j, STEP * (j + 1)):
+            pass_on(far, d, slot_f, 1)
+        table(0, distant, slot_f, STEP * j, STEP)
+    cost_b[cid, slot_h] = both[home, cid]
+    cost_b[cid, slot_f] = far[cid]
 
     def top_first():
         c, s = half[0, 0], half[0, 1]
@@ -133,51 +181,109 @@
 
         lax.fori_loop(0, ROWS // 8, rows, 0)
 
+    def low(layer, index):
+        xs = jnp.concatenate([work[k] for k in index], axis=0)
+        ys = jnp.dot(xs, mix[layer], precision=HIGHEST, preferred_element_type=jnp.float32)
+        ys = jnp.concatenate(
+            [jnp.concatenate([ys[i * 128:(i + 1) * 128, 0:128].T, ys[i * 128:(i + 1) * 128, 128:256].T], axis=1)
+             for i in range(len(index))], axis=0)
+        return jnp.dot(ys, mix[layer], precision=HIGHEST, preferred_element_type=jnp.float32)
+
     def low_and_send(layer):
         started = []
         for group in GROUPS:
-            index = [flip(bits, mask)[0] for mask in group]
-            x = jnp.concatenate([work[k] for k in index], axis=0)
-            y = jnp.dot(x, mix[layer], precision=HIGHEST, preferred_element_type=jnp.float32)
-            y = jnp.concatenate(
-                [jnp.concatenate([y[i * 128:(i + 1) * 128, 0:128].T, y[i * 128:(i + 1) * 128, 128:256].T], axis=1)
-                 for i in range(len(group))], axis=0)
-            y = jnp.dot(y, mix[layer], precision=HIGHEST, preferred_element_type=jnp.float32)
+            index = [cube_peer(mask)[0] for mask in group]
+            ys = low(layer, index)
             for i, mask in enumerate(group):
                 if mask:
-                    snd[layer, index[i]] = y[i * 128:(i + 1) * 128]
+                    snd[layer, index[i]] = ys[i * 128:(i + 1) * 128]
                 else:
-                    rcv[layer, me] = y[i * 128:(i + 1) * 128]
-            for mask in group:
+                    rcv[layer, cid] = ys[i * 128:(i + 1) * 128]
+            for i, mask in enumerate(group):
                 if mask:
-                    copy = copies(lambda peer: snd.at[layer, peer], rcv.at[layer, me], ss_sem.at[layer],
-                                  sr_sem.at[layer], mask)
+                    copy = remote(snd.at[layer, index[i]], rcv.at[layer, cid], ss_sem.at[layer, mask],
+                                  sr_sem.at[layer, mask], cube_peer(mask)[1])
                     copy.start()
                     started.append(copy)
         return started
 
-    table(0, lambda k: cost_ref[k])
+    last = LAYERS - 1
+
+    def final_copy(mask):
+        b, t, where = plane_peer(mask, h)
+        rows = pl.ds(pl.multiple_of(HALF * t, HALF), HALF)
+        return [remote(snd.at[last, b + 8 * k, rows], rcv.at[last, cid, HALF * k:HALF * (k + 1)],
+                       fs_sem.at[mask, k], fr_sem.at[(mask & 7) + 8 * x, k], where) for k in range(2)]
+
+    def low_and_return():
+        for pair in PAIRS:
+            index = [plane_peer(mask, h)[0] + 8 * k for mask in pair for k in range(2)]
+            ys = low(last, index)
+            for i in range(4):
+                snd[last, index[i]] = ys[i * 128:(i + 1) * 128]
+            for mask in pair:
+                for copy in final_copy(mask + 8):
+                    copy.start()
+        for pair in PAIRS:
+            for mask in pair:
+                if mask:
+                    for copy in final_copy(mask):
+                        copy.start()
+
+        @pl.when(home == 0)
+        def _():
+            for copy in final_copy(0):
+                copy.start()
+
+        @pl.when(home == 1)
+        def _():
+            b = plane_peer(0, h)[0]
+            for k in range(2):
+                rcv[last, cid, HALF * k:HALF * (k + 1)] = snd[last, b + 8 * k, slot_h]
+
     top_first()
     pending = low_and_send(0)
-    table(2, lambda k: cost_ref[k])
-    for copy in cost_copies:
-        copy.wait()
+    table(2, keep, slot_h, 0, BLOCKS)
+    table(2, distant, slot_f, 0, BLOCKS)
+    for mask in range(1, BLOCKS):
+        peer, where = cube_peer(mask)
+        for which, rows in enumerate((slot_h, slot_f)):
+            remote(far.at[peer], cost_b.at[peer, rows], cs_sem.at[which, peer], cr_sem.at[which, peer], where).wait()
 
     def turned(k):
         return cost_b[k].T
 
-    table(1, turned)
+    everything = pl.ds(0, ROWS)
+    table(1, turned, everything, 0, BLOCKS)
     for layer in range(1, LAYERS):
         if layer == 2:
-            table(3, turned)
+            table(3, turned, everything, 0, BLOCKS)
         for copy in pending:
             copy.wait()
         top(layer)
-        pending = low_and_send(layer)
-    for copy in pending:
-        copy.wait()
-
-    last = LAYERS - 1
+        pending = low_and_send(layer) if layer < last else low_and_return()
+    for copy in x_copies + z_copies:
+        copy.wait_send()
+    for mask in range(1, BLOCKS):
+        for copy in final_copy(mask):
+            copy.wait_send()
+
+    def arrived(m, v):
+        for k in range(2):
+            remote(snd.at[last, 0, 0:HALF], rcv.at[last, 0, 0:HALF], fs_sem.at[0, k], fr_sem.at[m + 8 * v, k],
+                   {'inst': 1 - x, 'qx': qx, 'qy': qy}).wait_recv()
+
+    for m in range(1, 8):
+        for v in range(2):
+            arrived(m, v)
+    arrived(0, 1 - x)
+
+    @pl.when(home == 0)
+    def _():
+        for copy in final_copy(0):
+            copy.wait_send()
+        arrived(0, x)
+
     c, s = half[last, 0], half[last, 1]
 
     def finish(r, acc):
@@ -190,8 +296,10 @@
             acc = acc + cost_ref[k, at, :] * (re * re + im * im)
         return acc
 
+    me = core + 2 * z0 + 4 * y + 8 * h
     part[me] = lax.fori_loop(0, ROWS // 8, finish, jnp.zeros((8, LANES), jnp.float32))
-    sums = [copies(lambda peer: part.at[me], part.at[me], es_sem, er_sem, mask) for mask in range(1, BLOCKS)]
+    sums = [remote(part.at[me], part.at[me], es_sem.at[mask], er_sem.at[mask], plane_peer(mask, x)[2])
+            for mask in range(1, BLOCKS)]
     for copy in sums:
         copy.start()
     for copy in sums:
@@ -220,6 +328,8 @@
             in_specs=[vmem, smem, smem],
             out_specs=(smem, vmem, vmem),
             scratch_shapes=[
+                pltpu.VMEM((2, BLOCKS, HALF, LANES), jnp.float32),
+                pltpu.VMEM((BLOCKS, HALF, LANES), jnp.float32),
                 pltpu.VMEM(block, jnp.float32),
                 pltpu.VMEM(pair, jnp.float32),
                 pltpu.VMEM((LAYERS,) + pair, jnp.float32),
@@ -228,8 +338,10 @@
                 pltpu.VMEM((LAYERS, 2 * LANES, 2 * LANES), jnp.float32),
                 pltpu.VMEM((LAYERS, 2, 8, LANES), jnp.float32),
                 pltpu.VMEM((BLOCKS, 8, LANES), jnp.float32),
-                dma((BLOCKS,)), dma((BLOCKS,)),
+                dma((CHUNKS,)), dma((CHUNKS,)), dma((CHUNKS,)), dma((CHUNKS,)),
+                dma((2, BLOCKS)), dma((2, BLOCKS)),
                 dma((LAYERS, BLOCKS)), dma((LAYERS, BLOCKS)),
+                dma((BLOCKS, 2)), dma((BLOCKS, 2)),
                 dma((BLOCKS,)), dma((BLOCKS,)),
             ],
             compiler_params=pltpu.CompilerParams(collective_id=0, has_side_effects=True),

time: 239 us -> 198 us (0.83)
  Pallas kernels: 233 us -> 192 us
    pallas_call x1, Pallas kernels: 233 us -> 192 us  [device_body(): pl.pallas_call(functools.partial(kernel, size), out_shape=(jax.ShapeDtype...]
where the time goes in v2:
time: 198 us
  Pallas kernels  192 us (97%)
  local copies, waits for them, and re-layouts  3.39 us (2%)
  between operations  2.39 us (1%)
    pallas_call x1, Pallas kernels, device_body(): pl.pallas_call(functools.partial(kernel, size), out_shape=(jax.ShapeDtype...  192 us

profile of v2, /device:TPU:0, one launch (start us, length us, event | category | flops | bytes accessed | tf_op | source)
XLA Modules:
  0.0 198.0 jit_solution(7630307407839065297)
XLA Ops:
  0.6 192.2 %qaoa.1 = (f32[1]{0:T(128)}, f32[16,128,128]{2,1,0:T(8,128)}, f32[16,128,128]{2,1,0:T(8,128)}) custom-call(f32[16,128,128]{2,1,0:T(8,128)} %bitcast.3, f32[4]{0:T(128)} %gam_ref.1, f32[4]{0:T(128)} %bet_ref.1), custom_call_target="tpu_custom_call" | custom-call | tf_op jit(solution)/shard_map/qaoa/pallas_call | solution.py:324
  193.5 0.0 copy-start
  193.5 2.4 %copy.10 = f32[262144]{0:T(1024)} copy(f32[262144]{0:T(1024)} %bitcast.5) | data formatting | bytes 2097152
  195.8 0.0 copy-done
  195.8 1.0 copy.11
Async XLA Ops:
  193.5 2.4 %copy-start = (f32[16,128,128]{2,1,0:T(8,128)S(1)}, f32[16,128,128]{2,1,0:T(8,128)}, u32[]{:S(2)}) copy-start(f32[16,128,128]{2,1,0:T(8,128)} %get-tuple-element.8) | copy-start | bytes 3145732
